TPU v7x, 512 devices: a whole 4x8x8 slice. The times are simulated.
512 devices in a mesh: win: 64 (over z, x, y_hi), strip: 8 (over y_lo, core).
Axes of the slice: x: 4, y: 8 (y_hi: 2, y_lo: 4; y = y_hi * 4 + y_lo), z: 8, core: 2. Of those that a mesh axis runs over, the one named last changes fastest.
Arguments:
- start_states: float32 [64, 3, 128, 1024], P('win', None, 'strip'), may hold values from -1.5 to 1.5
- obs_cells: int32 [64, 4, 2048], P('win', None, 'strip'), may hold values from 0 to 16383
- obs_values: float32 [64, 4, 2048], P('win', None, 'strip'), may hold values from -1.5 to 1.5
- weighting: float32 [3, 128, 128], replicated, may hold values from -0.5 to 0.5
- live_windows: int32 [64], P('win'), may hold values 0 or 1
Outputs:
- gradient: float32 [64, 3, 128, 1024], P('win', None, 'strip')
- analysis: float32 [64, 3, 128, 1024], P('win', None, 'strip')
Inputs may be any that keep to these rules, and one draw needn't show every extreme that they name: `obs_cells`: each entry indexes a cell of its own row strip as (row within the strip) * 1024 + column.
All inputs are finite; a program needn't handle non-finite values. No bound on the sum of `live_windows` on one device may be relied on, other than what follows from the above.
Results may differ from a plain program's by a relative error of at most 0.0003.
Values sent between devices are 32-bit elements; how exact they have to be, the bound alone decides.
No kernel may reach another device: no remote copies, remote signals or barrier semaphores. Data moves between devices by JAX's collectives and lax.ppermute only.
A program may use at most 64 MiB of HBM per device.

v0:
```python
import jax
import jax.numpy as jnp
from jax import lax
from jax.sharding import PartitionSpec as P

TIME_STEP = 0.2
DIFFUSION = 0.12
CORIOLIS = 0.5
STEP_LENGTH = 0.5


def from_behind(shard, axis, by):
    devices = lax.axis_size(axis)
    pairs = [(i, i + by) for i in range(devices) if 0 <= i + by < devices]
    return lax.ppermute(shard, axis, pairs)


def extended(shard, sides, width):
    for axis, dim in sides:
        devices, length = (lax.axis_size(axis), shard.shape[dim])
        up = [(i, (i + 1) % devices) for i in range(devices - 1)]
        down = [(j, i) for i, j in up]
        last = lax.slice_in_dim(shard, length - width, length, axis=dim)
        leading = lax.slice_in_dim(shard, 0, width, axis=dim)
        before = lax.ppermute(last, axis, up)
        after = lax.ppermute(leading, axis, down)
        shard = jnp.concatenate([before, shard, after], axis=dim)
    return shard


def col_diff(field):
    return (jnp.roll(field[1:-1], -1, 1) - jnp.roll(field[1:-1], 1, 1)) * 0.5


def row_diff(field):
    return (field[2:] - field[:-2]) * 0.5


def laplace(field):
    inner = field[1:-1]
    return field[2:] + field[:-2] + jnp.roll(inner, -1, 1) + jnp.roll(inner, 1, 1) - 4.0 * inner


def advance(padded):
    height, east_wind, north_wind = (padded[0], padded[1], padded[2])
    depth = 1.0 + height
    flux_east = east_wind * depth
    flux_north = north_wind * depth
    height_in, east_in, north_in = (height[1:-1], east_wind[1:-1], north_wind[1:-1])
    new_height = (
        height_in
        - TIME_STEP * (col_diff(flux_east) + row_diff(flux_north))
        + DIFFUSION * laplace(height)
    )
    new_east = (
        east_in
        - TIME_STEP
        * (col_diff(height) + east_in * col_diff(east_wind) + north_in * row_diff(east_wind))
        + TIME_STEP * CORIOLIS * north_in
        + DIFFUSION * laplace(east_wind)
    )
    new_north = (
        north_in
        - TIME_STEP
        * (row_diff(height) + east_in * col_diff(north_wind) + north_in * row_diff(north_wind))
        - TIME_STEP * CORIOLIS * east_in
        + DIFFUSION * laplace(north_wind)
    )
    return jnp.stack([new_height, new_east, new_north])


def weigh(defect, weighting):
    fields, rows, cols = defect.shape
    width = weighting.shape[1]
    blocks = defect.reshape(fields, rows, cols // width, width)
    mixed = jnp.einsum("frbi,fij->frbj", blocks, weighting, precision=lax.Precision.HIGHEST)
    return defect + mixed.reshape(fields, rows, cols)


def forcing(adjoint, state, cells, values, alive, read_rows, write_rows):
    cols = state.shape[2]
    source = state[0].reshape(state.shape[1] * cols)
    innovation = (source[cells + read_rows * cols] - values) * alive
    target = adjoint[0].reshape(adjoint.shape[1] * cols)
    target = target.at[cells + write_rows * cols].add(innovation)
    return adjoint.at[0].set(target.reshape(adjoint.shape[1], cols))


def inside_map(field, strip_base, total_rows, margin):
    rows_here = field.shape[1]
    row_ids = strip_base - margin + jnp.arange(rows_here)
    inside = (row_ids >= 0) & (row_ids < total_rows)
    return jnp.where(inside[None, :, None], field, 0.0)


def per_device(start_states, obs_cells, obs_values, weighting, live_windows):
    state = start_states[0]
    cells = obs_cells[0]
    values = obs_values[0]
    rows = state.shape[1]
    steps = cells.shape[0]
    strip_base = lax.axis_index("strip") * rows
    total_rows = rows * lax.axis_size("strip")
    alive = live_windows[0].astype(state.dtype)
    is_last = lax.axis_index("win") == lax.axis_size("win") - 1
    next_start = from_behind(state, "win", -1)
    trajectory = []
    wide = extended(state, (("strip", 1),), steps)
    for moment in range(steps):
        trajectory.append(wide)
        wide = advance(wide)
        margin = steps - moment - 1
        if margin > 0:
            wide = inside_map(wide, strip_base, total_rows, margin)
    previous_end = from_behind(wide, "win", 1)
    own_weighted = weigh(state - previous_end, weighting)
    next_weighted = jnp.where(is_last, 0.0, weigh(next_start - wide, weighting))
    adjoint = forcing(-next_weighted, wide, cells[steps - 1], values[steps - 1], alive, 0, 0)
    for moment in range(steps - 1, -1, -1):
        unused, pullback = jax.vjp(advance, trajectory[moment])
        adjoint = pullback(adjoint)[0]
        margin = steps - moment
        adjoint = inside_map(adjoint, strip_base, total_rows, margin)
        if moment > 0:
            adjoint = forcing(
                adjoint,
                trajectory[moment],
                cells[moment - 1],
                values[moment - 1],
                alive,
                margin,
                margin,
            )
    spill = jnp.concatenate([adjoint[:, :steps], adjoint[:, steps + rows :]], axis=1)
    received = extended(spill, (("strip", 1),), steps)
    owned = adjoint[:, steps : steps + rows]
    owned = owned.at[:, :steps].add(received[:, :steps])
    owned = owned.at[:, rows - steps :].add(received[:, 3 * steps :])
    adjoint = owned
    gradient = own_weighted + adjoint
    analysis = state - STEP_LENGTH * gradient
    return (gradient[None], analysis[None])


def solution(mesh):
    placed = (
        P("win", None, "strip", None),
        P("win", None, "strip"),
        P("win", None, "strip"),
        P(),
        P("win"),
    )
    return jax.shard_map(
        per_device,
        mesh=mesh,
        in_specs=placed,
        out_specs=(P("win", None, "strip", None), P("win", None, "strip", None)),
        check_vma=False,
    )
```

profile of v0, /device:TPU:257, one launch (start us, length us, event | category | flops | bytes accessed | tf_op | source)
XLA Modules:
  0.0 105.7 jit_solution(6369137391221737079)
XLA Ops:
  0.7 8.9 %collective-permute-start.3 = (f32[3,16,1024]{2,1,0:T(8,128)}, f32[3,16,1024]{2,1,0:T(8,128)S(1)}, u32[]{:S(2)}, u32[]{:S(2)}) collective-permute-start(f32[3,16,1024]{2,1,0:T(8,128)} %bitcast.608), channel_id=1, source_target_pairs={{8,0},{16,8},{24,16},{32,24},{40,32},{48,40},{56,48},{64,56},{72,6... | collective-permute-start | bytes 589832 | tf_op jit(solution)/shard_map/ppermute | solution.py:15
  9.5 1.0 fusion.161
  10.5 3.1 %collective-permute-start = (f32[3,4,1024]{2,1,0:T(4,128)S(1)}, f32[3,4,1024]{2,1,0:T(4,128)S(1)}, u32[]{:S(2)}, u32[]{:S(2)}) collective-permute-start(f32[3,4,1024]{2,1,0:T(4,128)S(1)} %get-tuple-element.232), channel_id=1, source_target_pairs={{0,1},{1,2},{2,3},{3,4},{4,5},{5,6},{6,7},{8,9},{9,10},{10,11},{11... | collective-permute-start | bytes 147464 | tf_op jit(solution)/shard_map/ppermute | solution.py:25
  13.6 1.9 %collective-permute-start.1 = (f32[3,4,1024]{2,1,0:T(4,128)S(1)}, f32[3,4,1024]{2,1,0:T(4,128)S(1)}, u32[]{:S(2)}, u32[]{:S(2)}) collective-permute-start(f32[3,4,1024]{2,1,0:T(4,128)S(1)} %get-tuple-element.233), channel_id=1, source_target_pairs={{1,0},{2,1},{3,2},{4,3},{5,4},{6,5},{7,6},{9,8},{10,9},{11,10},{12... | collective-permute-start | bytes 147464 | tf_op jit(solution)/shard_map/ppermute | solution.py:26
  15.7 0.6 copy-done.47
  18.6 1.5 %collective-permute-done.1 = f32[3,4,1024]{2,1,0:T(4,128)S(1)} collective-permute-done((f32[3,4,1024]{2,1,0:T(4,128)S(1)}, f32[3,4,1024]{2,1,0:T(4,128)S(1)}, u32[]{:S(2)}, u32[]{:S(2)}) %collective-permute-start.1) | collective-permute-done | bytes 49184 | tf_op jit(solution)/shard_map/ppermute | solution.py:26
  20.2 0.7 fusion.166
  21.1 0.7 fusion.168
  22.9 0.7 fusion.176
  23.7 0.7 fusion.179
  24.5 0.7 fusion.178
  25.9 0.7 fusion.187
  26.7 0.7 fusion.186
  27.5 0.7 fusion.189
  28.2 0.7 fusion.188
  29.7 0.7 fusion.211
  30.6 0.7 fusion.213
  31.3 0.7 fusion.212
  32.1 0.9 slice-done.2
  33.0 0.9 slice-done.1
  33.9 0.9 slice-done
  34.8 1.7 %gather_fusion = f32[256]{0:T(256)S(1)} fusion(f32[16384]{0:T(1024)S(1)} %bitcast.607, s32[1024]{0:T(1024)S(1)} %pad_clamp_fusion.3), kind=kCustom, calls=%fused_computation | custom fusion | bytes 3072 | tf_op jit(solution)/shard_map/gather | solution.py:83
  36.5 1.7 %gather_fusion.1 = f32[256]{0:T(256)S(1)} fusion(f32[18432]{0:T(1024)S(1)} %reshape_squeeze.23, s32[1024]{0:T(1024)S(1)} %pad_clamp_fusion.2), kind=kCustom, calls=%fused_computation.1 | custom fusion | bytes 3072 | tf_op jit(solution)/shard_map/gather | solution.py:83
  38.9 1.7 %gather_fusion.2 = f32[256]{0:T(256)S(1)} fusion(f32[20480]{0:T(1024)S(1)} %reshape_squeeze.25, s32[1024]{0:T(1024)S(1)} %pad_clamp_fusion.1), kind=kCustom, calls=%fused_computation.2 | custom fusion | bytes 3072 | tf_op jit(solution)/shard_map/gather | solution.py:83
  41.1 1.7 %gather_fusion.3 = f32[256]{0:T(256)S(1)} fusion(f32[22528]{0:T(1024)S(1)} %reshape_squeeze.27, s32[1024]{0:T(1024)S(1)} %pad_clamp_fusion), kind=kCustom, calls=%fused_computation.3 | custom fusion | bytes 3072 | tf_op jit(solution)/shard_map/gather | solution.py:83
  43.6 0.7 pad_maximum_fusion.1
  45.9 2.0 %scatter_fusion = f32[16384]{0:T(1024)S(1)} fusion(f32[16384]{0:T(1024)S(1)} %bitcast.606, s32[256]{0:T(256)S(1)} %bitcast.640, f32[256]{0:T(256)S(1)} %subtract_multiply_fusion.11), kind=kCustom, calls=%fused_computation.4 | custom fusion | flops 256 | bytes 4096 | tf_op jit(solution)/shard_map/scatter-add | solution.py:85
  49.8 0.7 copy-done.14
  51.4 0.9 copy-done.4
  53.3 0.7 fusion.185
  54.0 0.6 copy-done.42
  54.7 2.1 %scatter_fusion.1 = f32[18432]{0:T(1024)S(1)} fusion(f32[18432]{0:T(1024)S(1)} %reshape_squeeze.22, s32[256]{0:T(256)S(1)} %bitcast.638, f32[256]{0:T(256)} %subtract_multiply_fusion.10), kind=kCustom, calls=%fused_computation.5 | custom fusion | flops 256 | bytes 4096 | tf_op jit(solution)/shard_map/scatter-add | solution.py:85
  57.3 0.7 copy-done.18
  58.5 0.6 copy-done.21
  60.2 0.7 copy-done.10
  61.9 0.9 copy-done.2
  63.8 0.7 fusion.175
  65.2 2.1 %scatter_fusion.2 = f32[20480]{0:T(1024)S(1)} fusion(f32[20480]{0:T(1024)S(1)} %reshape_squeeze.24, s32[256]{0:T(256)S(1)} %bitcast.636, f32[256]{0:T(256)S(1)} %copy-done.46), kind=kCustom, calls=%fused_computation.6 | custom fusion | flops 256 | bytes 4096 | tf_op jit(solution)/shard_map/scatter-add | solution.py:85
  67.9 0.7 copy-done.20
  69.1 0.6 copy-done.22
  70.7 0.7 copy-done.8
  73.7 2.0 %scatter_fusion.3 = f32[22528]{0:T(1024)S(1)} fusion(f32[22528]{0:T(1024)S(1)} %reshape_squeeze.26, s32[256]{0:T(256)S(1)} %bitcast.634, f32[256]{0:T(256)S(1)} %copy-done.45), kind=kCustom, calls=%fused_computation.7 | custom fusion | flops 256 | bytes 4096 | tf_op jit(solution)/shard_map/scatter-add | solution.py:85
  79.3 3.1 %collective-permute-start.4 = (f32[3,4,1024]{2,1,0:T(4,128)S(1)}, f32[3,4,1024]{2,1,0:T(4,128)S(1)}, u32[]{:S(2)}, u32[]{:S(2)}) collective-permute-start(f32[3,4,1024]{2,1,0:T(4,128)S(1)} %get-tuple-element.137), channel_id=1, source_target_pairs={{0,1},{1,2},{2,3},{3,4},{4,5},{5,6},{6,7},{8,9},{9,10},{10,11},{11... | collective-permute-start | bytes 147464 | tf_op jit(solution)/shard_map/ppermute | solution.py:25
  82.4 1.9 %collective-permute-start.5 = (f32[3,4,1024]{2,1,0:T(4,128)S(1)}, f32[3,4,1024]{2,1,0:T(4,128)S(1)}, u32[]{:S(2)}, u32[]{:S(2)}) collective-permute-start(f32[3,4,1024]{2,1,0:T(4,128)S(1)} %get-tuple-element.136), channel_id=1, source_target_pairs={{1,0},{2,1},{3,2},{4,3},{5,4},{6,5},{7,6},{9,8},{10,9},{11,10},{12... | collective-permute-start | bytes 147464 | tf_op jit(solution)/shard_map/ppermute | solution.py:26
  84.4 1.9 %collective-permute-start.2 = (f32[3,16,1024]{2,1,0:T(8,128)S(1)}, f32[3,16,1024]{2,1,0:T(8,128)S(1)}, u32[]{:S(2)}, u32[]{:S(2)}) collective-permute-start(f32[3,16,1024]{2,1,0:T(8,128)S(1)} %copy-done.17), channel_id=1, source_target_pairs={{0,8},{8,16},{16,24},{24,32},{32,40},{40,48},{48,56},{56,64},{64,7... | collective-permute-start | bytes 589832 | tf_op jit(solution)/shard_map/ppermute | solution.py:15
  86.3 1.5 %collective-permute-done.5 = f32[3,4,1024]{2,1,0:T(4,128)S(1)} collective-permute-done((f32[3,4,1024]{2,1,0:T(4,128)S(1)}, f32[3,4,1024]{2,1,0:T(4,128)S(1)}, u32[]{:S(2)}, u32[]{:S(2)}) %collective-permute-start.5) | collective-permute-done | bytes 49184 | tf_op jit(solution)/shard_map/ppermute | solution.py:26
  87.9 16.6 %collective-permute-done.2 = f32[3,16,1024]{2,1,0:T(8,128)S(1)} collective-permute-done((f32[3,16,1024]{2,1,0:T(8,128)S(1)}, f32[3,16,1024]{2,1,0:T(8,128)S(1)}, u32[]{:S(2)}, u32[]{:S(2)}) %collective-permute-start.2) | collective-permute-done | bytes 196640 | tf_op jit(solution)/shard_map/ppermute | solution.py:15
  104.9 0.8 subtract_bitcast_fusion
  (329 shorter events, 24.9 us)
Async XLA Ops:
  0.6 43.7 %copy-start = (f32[3,128,128]{2,1,0:T(8,128)S(1)}, f32[3,128,128]{2,1,0:T(8,128)}, u32[]{:S(2)}) copy-start(f32[3,128,128]{2,1,0:T(8,128)} %param.20) | copy-start | bytes 589828
  0.6 19.4 %copy-start.7 = (f32[1,3,16,1024]{3,2,1,0:T(8,128)S(1)}, f32[1,3,16,1024]{3,2,1,0:T(8,128)}, u32[]{:S(2)}) copy-start(f32[1,3,16,1024]{3,2,1,0:T(8,128)} %param.17) | copy-start | bytes 589828
  0.7 42.9 %collective-permute-start.3 = (f32[3,16,1024]{2,1,0:T(8,128)}, f32[3,16,1024]{2,1,0:T(8,128)S(1)}, u32[]{:S(2)}, u32[]{:S(2)}) collective-permute-start(f32[3,16,1024]{2,1,0:T(8,128)} %bitcast.608), channel_id=1, source_target_pairs={{8,0},{16,8},{24,16},{32,24},{40,32},{48,40},{56,48},{64,56},{72,6... | collective-permute-start | bytes 589832 | tf_op jit(solution)/shard_map/ppermute | solution.py:15
  10.5 8.1 %collective-permute-start = (f32[3,4,1024]{2,1,0:T(4,128)S(1)}, f32[3,4,1024]{2,1,0:T(4,128)S(1)}, u32[]{:S(2)}, u32[]{:S(2)}) collective-permute-start(f32[3,4,1024]{2,1,0:T(4,128)S(1)} %get-tuple-element.232), channel_id=1, source_target_pairs={{0,1},{1,2},{2,3},{3,4},{4,5},{5,6},{6,7},{8,9},{9,10},{10,11},{11... | collective-permute-start | bytes 147464 | tf_op jit(solution)/shard_map/ppermute | solution.py:25
  13.6 6.4 %collective-permute-start.1 = (f32[3,4,1024]{2,1,0:T(4,128)S(1)}, f32[3,4,1024]{2,1,0:T(4,128)S(1)}, u32[]{:S(2)}, u32[]{:S(2)}) collective-permute-start(f32[3,4,1024]{2,1,0:T(4,128)S(1)} %get-tuple-element.233), channel_id=1, source_target_pairs={{1,0},{2,1},{3,2},{4,3},{5,4},{6,5},{7,6},{9,8},{10,9},{11,10},{12... | collective-permute-start | bytes 147464 | tf_op jit(solution)/shard_map/ppermute | solution.py:26
  15.6 6.7 %copy-start.49 = (pred[22]{0:T(512)(128)(4,1)}, pred[22]{0:T(512)(128)(4,1)S(1)}, u32[]{:S(2)}) copy-start(pred[22]{0:T(512)(128)(4,1)S(1)} %compare_and_fusion.1) | copy-start | bytes 70
  15.6 9.8 %copy-start.51 = (pred[20]{0:T(512)(128)(4,1)}, pred[20]{0:T(512)(128)(4,1)S(1)}, u32[]{:S(2)}) copy-start(pred[20]{0:T(512)(128)(4,1)S(1)} %compare_and_fusion.2) | copy-start | bytes 64
  16.3 12.9 %copy-start.53 = (pred[18]{0:T(512)(128)(4,1)}, pred[18]{0:T(512)(128)(4,1)S(1)}, u32[]{:S(2)}) copy-start(pred[18]{0:T(512)(128)(4,1)S(1)} %compare_and_fusion.3) | copy-start | bytes 58
  16.3 0.7 copy-start.41
  16.3 0.7 copy-start.39
  16.3 0.7 copy-start.37
  22.4 9.6 %copy-start.1 = (f32[3,22,1024]{2,1,0:T(8,128)}, f32[3,22,1024]{2,1,0:T(8,128)S(1)}, u32[]{:S(2)}) copy-start(f32[3,22,1024]{2,1,0:T(8,128)S(1)} %maximum_select_fusion) | copy-start | bytes 811012
  25.5 6.5 %copy-start.3 = (f32[3,20,1024]{2,1,0:T(8,128)}, f32[3,20,1024]{2,1,0:T(8,128)S(1)}, u32[]{:S(2)}) copy-start(f32[3,20,1024]{2,1,0:T(8,128)S(1)} %maximum_select_fusion.1) | copy-start | bytes 737284
  29.3 2.7 %copy-start.5 = (f32[3,18,1024]{2,1,0:T(8,128)}, f32[3,18,1024]{2,1,0:T(8,128)S(1)}, u32[]{:S(2)}) copy-start(f32[3,18,1024]{2,1,0:T(8,128)S(1)} %maximum_select_fusion.2) | copy-start | bytes 663556
  32.1 0.9 slice-start.2
  33.0 0.9 slice-start.1
  33.9 0.9 slice-start
  41.1 1.7 %copy-start.6 = (f32[3,18,1024]{2,1,0:T(8,128)S(1)}, f32[3,18,1024]{2,1,0:T(8,128)}, u32[]{:S(2)}) copy-start(f32[3,18,1024]{2,1,0:T(8,128)} %copy-done.5) | copy-start | bytes 663556
  49.6 0.8 copy-start.14
  49.6 0.9 copy-start.15
  49.7 0.9 copy-start.16
  49.7 0.9 copy-start.36
  49.8 0.8 copy-start.35
  51.3 1.0 copy-start.4
  58.5 0.7 copy-start.21
  60.0 0.9 copy-start.10
  60.0 0.9 copy-start.11
  60.0 1.0 copy-start.12
  60.0 1.0 copy-start.13
  60.0 1.0 copy-start.32
  60.0 1.0 copy-start.33
  60.0 1.0 copy-start.34
  60.2 0.8 copy-start.31
  61.8 1.0 copy-start.2
  67.9 0.7 copy-start.20
  69.0 0.7 copy-start.22
  70.5 0.9 copy-start.8
  70.6 0.9 copy-start.9
  70.6 0.9 copy-start.28
  70.6 0.9 copy-start.29
  70.6 0.9 copy-start.30
  70.7 0.8 copy-start.27
  77.5 0.7 copy-start.25
  77.5 0.7 copy-start.26
  79.3 5.0 %copy-start.17 = (f32[3,16,1024]{2,1,0:T(8,128)S(1)}, f32[3,16,1024]{2,1,0:T(8,128)}, u32[]{:S(2)}) copy-start(f32[3,16,1024]{2,1,0:T(8,128)} %get-tuple-element.213) | copy-start | bytes 589828
  79.3 7.0 %collective-permute-start.4 = (f32[3,4,1024]{2,1,0:T(4,128)S(1)}, f32[3,4,1024]{2,1,0:T(4,128)S(1)}, u32[]{:S(2)}, u32[]{:S(2)}) collective-permute-start(f32[3,4,1024]{2,1,0:T(4,128)S(1)} %get-tuple-element.137), channel_id=1, source_target_pairs={{0,1},{1,2},{2,3},{3,4},{4,5},{5,6},{6,7},{8,9},{9,10},{10,11},{11... | collective-permute-start | bytes 147464 | tf_op jit(solution)/shard_map/ppermute | solution.py:25
  82.4 5.4 %collective-permute-start.5 = (f32[3,4,1024]{2,1,0:T(4,128)S(1)}, f32[3,4,1024]{2,1,0:T(4,128)S(1)}, u32[]{:S(2)}, u32[]{:S(2)}) collective-permute-start(f32[3,4,1024]{2,1,0:T(4,128)S(1)} %get-tuple-element.136), channel_id=1, source_target_pairs={{1,0},{2,1},{3,2},{4,3},{5,4},{6,5},{7,6},{9,8},{10,9},{11,10},{12... | collective-permute-start | bytes 147464 | tf_op jit(solution)/shard_map/ppermute | solution.py:26
  84.4 20.1 %collective-permute-start.2 = (f32[3,16,1024]{2,1,0:T(8,128)S(1)}, f32[3,16,1024]{2,1,0:T(8,128)S(1)}, u32[]{:S(2)}, u32[]{:S(2)}) collective-permute-start(f32[3,16,1024]{2,1,0:T(8,128)S(1)} %copy-done.17), channel_id=1, source_target_pairs={{0,8},{8,16},{16,24},{24,32},{32,40},{40,48},{48,56},{56,64},{64,7... | collective-permute-start | bytes 589832 | tf_op jit(solution)/shard_map/ppermute | solution.py:15
  (17 other events, 11.2 us)
where the time goes:
time: 107 us; the launch traced here: 106 us
  local copies, waits for them, and re-layouts  41.1 us (38%)
  starting transfers between devices  20.8 us (19%)
  other arithmetic  20.4 us (19%)
  waiting for transfers between devices  19.7 us (18%)
  between operations  2.92 us (3%)
    ppermute x2, waiting for transfers between devices, from_behind(): return lax.ppermute(shard, axis, pairs)  16.6 us
    unnamed x117, local copies, waits for them, and re-layouts  13.6 us
    ppermute x2, starting transfers between devices, from_behind(): return lax.ppermute(shard, axis, pairs)  10.8 us
    slice x24, local copies, waits for them, and re-layouts, col_diff(): return (jnp.roll(field[1:-1], -1, 1) - jnp.roll(field[1:-1], 1, 1)) * 0.5  9.38 us
    scatter-add x4, other arithmetic, forcing(): target = target.at[cells + write_rows * cols].add(innovation)  8.19 us
    gather x4, local copies, waits for them, and re-layouts, forcing(): innovation = (source[cells + read_rows * cols] - values) * alive  6.88 us
    ppermute x2, starting transfers between devices, extended(): before = lax.ppermute(last, axis, up)  6.22 us
    ppermute x2, starting transfers between devices, extended(): after = lax.ppermute(leading, axis, down)  3.84 us
  transfers between devices with their start and end apart: 6, of which 4 were waited for; matrix products, arithmetic and copies ran while one was open for 21% of the time, Pallas kernels for 0%

commit v1 on v0

v1 whole, which is shorter than its diff:
```python
import jax
import jax.numpy as jnp
from jax import lax
from jax.experimental import pallas as pl
from jax.experimental.pallas import tpu as pltpu
from jax.sharding import PartitionSpec as P

TIME_STEP = 0.2
DIFFUSION = 0.12
CORIOLIS = 0.5
STEP_LENGTH = 0.5
LANES = 128
HALF_STEP = 0.5 * TIME_STEP
CENTRE = 1.0 - 4.0 * DIFFUSION
TURN = TIME_STEP * CORIOLIS


def neighbours(load, blocks, with_rows=True):
    kept = {}

    def block(b):
        key = ("c", b % blocks)
        if key not in kept:
            kept[key] = load(b % blocks)
        return kept[key]

    def turned(b, by):
        key = ("t", b % blocks, by)
        if key not in kept:
            kept[key] = pltpu.roll(block(b), by, 1)
        return kept[key]

    def get(b):
        here = block(b)
        lane = lax.broadcasted_iota(jnp.int32, here.shape, 1)
        before = jnp.where(lane == 0, turned(b - 1, 1), turned(b, 1))
        after = jnp.where(lane == LANES - 1, turned(b + 1, LANES - 1), turned(b, LANES - 1))
        above = pltpu.roll(here, 1, 0)
        below = pltpu.roll(here, here.shape[0] - 1, 0)
        return here, before, after, above, below

    return get


def columns(b):
    return pl.ds(b * LANES, LANES)


def step_forward(source, blocks, store):
    fields = [neighbours(lambda b, f=f: source(f, b), blocks) for f in range(3)]
    for b in range(blocks):
        h, hl, hr, hu, hd = fields[0](b)
        e, el, er, eu, ed = fields[1](b)
        n, nl, nr, nu, nd = fields[2](b)
        flux = (er + er * hr) - (el + el * hl) + (nd + nd * hd) - (nu + nu * hu)
        new_h = CENTRE * h - HALF_STEP * flux + DIFFUSION * ((hl + hr) + (hu + hd))
        grad_e = (hr - hl) + e * (er - el) + n * (ed - eu)
        new_e = CENTRE * e - HALF_STEP * grad_e + TURN * n + DIFFUSION * ((el + er) + (eu + ed))
        grad_n = (hd - hu) + e * (nr - nl) + n * (nd - nu)
        new_n = CENTRE * n - HALF_STEP * grad_n - TURN * e + DIFFUSION * ((nl + nr) + (nu + nd))
        store(b, (new_h, new_e, new_n))


def step_back(state, adjoint, blocks, store):
    winds = [neighbours(lambda b, f=f: state(f, b), blocks) for f in (1, 2)]
    parts = [neighbours(lambda b, f=f: adjoint(f, b), blocks) for f in range(3)]
    for b in range(blocks):
        h = state(0, b)
        e, el, er, eu, ed = winds[0](b)
        n, nl, nr, nu, nd = winds[1](b)
        p, pl_, pr, pu, pd = parts[0](b)
        q, ql, qr, qu, qd = parts[1](b)
        r, rl, rr, ru, rd = parts[2](b)
        p_col = pr - pl_
        p_row = pd - pu
        depth = 1.0 + h
        got_h = e * p_col + n * p_row + (qr - ql) + (rd - ru)
        new_h = CENTRE * p + HALF_STEP * got_h + DIFFUSION * ((pl_ + pr) + (pu + pd))
        got_e = (
            depth * p_col
            + (er * qr - el * ql)
            + (nd * qd - nu * qu)
            - q * (er - el)
            - r * (nr - nl)
        )
        new_e = CENTRE * q + HALF_STEP * got_e - TURN * r + DIFFUSION * ((ql + qr) + (qu + qd))
        got_n = (
            depth * p_row
            + (er * rr - el * rl)
            + (nd * rd - nu * ru)
            - q * (ed - eu)
            - r * (nd - nu)
        )
        new_n = CENTRE * r + HALF_STEP * got_n + TURN * q + DIFFUSION * ((rl + rr) + (ru + rd))
        store(b, (new_h, new_e, new_n))


def halves(x):
    high = x.astype(jnp.bfloat16)
    return high, (x - high.astype(jnp.float32)).astype(jnp.bfloat16)


def weigh(defect, weights, field, blocks):
    rows = defect[0].shape[0]
    stacked = jnp.concatenate(defect, axis=0)
    high, low = halves(stacked)
    product = jnp.dot(
        jnp.concatenate([high, low], axis=0), weights[field], preferred_element_type=jnp.float32
    )
    tall = rows * blocks
    mixed = (product[:tall, :LANES] + product[:tall, LANES:]) + (
        product[tall:, :LANES] + product[tall:, LANES:]
    )
    return [defect[b] + mixed[b * rows : (b + 1) * rows] for b in range(blocks)]


def inside_mask(width):
    strip = lax.axis_index("strip")
    row = lax.broadcasted_iota(jnp.int32, (8, width), 0)
    first = strip == 0
    last = strip == lax.axis_size("strip") - 1
    outside = ((row < 4) & last) | ((row >= 4) & first)
    return jnp.where(outside, 0.0, 1.0)


def observe_kernel(rows, blocks, cells, values, live, weighting, counts, sums, weights):
    steps, seen = cells.shape[1:]
    alive = live[0].astype(jnp.float32)
    for field in range(3):
        high, low = halves(weighting[field])
        weights[field] = jnp.concatenate([high, low], axis=1)
    cols_bits = LANES.bit_length() - 1
    col_blocks = blocks.bit_length() - 1
    for j in range(steps):
        cell = cells[0, j : j + 1, :]
        place = ((cell >> cols_bits) & (blocks - 1)) * rows + (cell >> (cols_bits + col_blocks))
        lane = cell & (LANES - 1)
        value = values[0, j : j + 1, :]
        tall = lax.broadcasted_iota(jnp.int32, (rows * blocks, seen), 0)
        wide = lax.broadcasted_iota(jnp.int32, (LANES, seen), 0)
        at_place = tall == place
        left = [jnp.where(at_place, 1.0, 0.0).astype(jnp.bfloat16)]
        rest = value
        for part in range(3):
            piece = rest.astype(jnp.bfloat16).astype(jnp.float32)
            left.append(jnp.where(at_place, piece, 0.0).astype(jnp.bfloat16))
            rest = rest - piece
        right = jnp.where(wide == lane, 1.0, 0.0).astype(jnp.bfloat16)
        product = lax.dot_general(
            jnp.concatenate(left, axis=0),
            right,
            (((1,), (1,)), ((), ())),
            preferred_element_type=jnp.float32,
        )
        size = rows * blocks
        count = product[:size] * alive
        total = (product[size : 2 * size] + product[2 * size : 3 * size] + product[3 * size :]) * alive
        for b in range(blocks):
            counts[j, :, columns(b)] = count[b * rows : (b + 1) * rows]
            sums[j, :, columns(b)] = total[b * rows : (b + 1) * rows]


def forward_kernel(rows, blocks, steps, start, above, below, counts, path, end):
    width = blocks * LANES
    mask = inside_mask(LANES)
    for f in range(3):
        path[0, f, 0:rows, :] = start[0, f]
        path[0, f, rows : rows + 4, :] = below[f]
        path[0, f, rows + 4 : rows + 8, :] = above[f]

    def advance(j, _):
        def store(b, new):
            for f in range(3):
                path[j + 1, f, 0:rows, columns(b)] = new[f][:rows]
                path[j + 1, f, rows : rows + 8, columns(b)] = new[f][rows:] * mask

        step_forward(lambda f, b: path[j, f, :, columns(b)], blocks, store)
        return 0

    lax.fori_loop(0, steps - 1, advance, 0)

    def store_end(b, new):
        for f in range(3):
            end[f, :, columns(b)] = new[f][:rows]

    step_forward(lambda f, b: path[steps - 1, f, :, columns(b)], blocks, store_end)


def adjoint_kernel(
    rows, blocks, steps, path, end, next_start, counts, sums, weights, own, to_next, to_prev, work
):
    mask = inside_mask(LANES)
    is_last = lax.axis_index("win") == lax.axis_size("win") - 1
    sign = jnp.where(is_last, 0.0, -1.0)
    for f in range(3):
        defect = [
            next_start[f, :, columns(b)] - end[f, :, columns(b)] for b in range(blocks)
        ]
        weighted = weigh(defect, weights, f, blocks)
        for b in range(blocks):
            start = weighted[b] * sign
            if f == 0:
                start = start + (
                    counts[steps - 1, :, columns(b)] * end[0, :, columns(b)]
                    - sums[steps - 1, :, columns(b)]
                )
            work[0, f, 0:rows, columns(b)] = start
            work[0, f, rows : rows + 8, columns(b)] = jnp.zeros((8, LANES), jnp.float32)

    def pull(i, _):
        j = steps - 1 - i

        def store(b, new):
            for f in range(3):
                mine = new[f][:rows]
                if f == 0:
                    mine = mine + (
                        counts[j - 1, :, columns(b)] * path[j, 0, 0:rows, columns(b)]
                        - sums[j - 1, :, columns(b)]
                    )
                work[i + 1, f, 0:rows, columns(b)] = mine
                work[i + 1, f, rows : rows + 8, columns(b)] = new[f][rows:] * mask

        step_back(
            lambda f, b: path[j, f, :, columns(b)],
            lambda f, b: work[i, f, :, columns(b)],
            blocks,
            store,
        )
        return 0

    lax.fori_loop(0, steps - 1, pull, 0)

    def store_own(b, new):
        for f in range(3):
            own[f, :, columns(b)] = new[f][:rows]
            to_next[f, :, columns(b)] = new[f][rows : rows + 4]
            to_prev[f, :, columns(b)] = new[f][rows + 4 :]

    step_back(
        lambda f, b: path[0, f, :, columns(b)],
        lambda f, b: work[steps - 1, f, :, columns(b)],
        blocks,
        store_own,
    )


def final_kernel(
    rows, blocks, start, previous_end, own, from_prev, from_next, weights, gradient, analysis
):
    for f in range(3):
        defect = [
            start[0, f, :, columns(b)] - previous_end[f, :, columns(b)] for b in range(blocks)
        ]
        weighted = weigh(defect, weights, f, blocks)
        for b in range(blocks):
            spill = jnp.concatenate(
                [
                    from_prev[f, :, columns(b)],
                    jnp.zeros((rows - 8, LANES), jnp.float32),
                    from_next[f, :, columns(b)],
                ],
                axis=0,
            )
            total = weighted[b] + own[f, :, columns(b)] + spill
            gradient[0, f, :, columns(b)] = total
            analysis[0, f, :, columns(b)] = start[0, f, :, columns(b)] - STEP_LENGTH * total


def call(body, outs, flops, in_specs=None, scratch=(), name=None):
    extra = {} if in_specs is None else {"in_specs": in_specs}
    return pl.pallas_call(
        body,
        out_shape=outs,
        scratch_shapes=list(scratch),
        compiler_params=pltpu.CompilerParams(vmem_limit_bytes=12 * 1024 * 1024),
        cost_estimate=pl.CostEstimate(flops=flops, bytes_accessed=1000000, transcendentals=0),
        name=name,
        **extra,
    )


def per_device(start_states, obs_cells, obs_values, weighting, live_windows):
    fields, rows, cols = start_states.shape[1:]
    steps = obs_cells.shape[1]
    blocks = cols // LANES
    frame = rows + 8
    f32 = jnp.float32
    shape = jax.ShapeDtypeStruct
    strips, windows = lax.axis_size("strip"), lax.axis_size("win")
    up = [(i, i + 1) for i in range(strips - 1)]
    down = [(j, i) for i, j in up]
    state = start_states[0]

    next_start = lax.ppermute(state, "win", [(i + 1, i) for i in range(windows - 1)])
    above = lax.ppermute(state[:, rows - 4 :], "strip", up)
    below = lax.ppermute(state[:, :4], "strip", down)

    whole = pl.BlockSpec(memory_space=pltpu.VMEM)
    counts, sums, weights = call(
        lambda *refs: observe_kernel(rows, blocks, *refs),
        (
            shape((steps, rows, cols), f32),
            shape((steps, rows, cols), f32),
            shape((fields, LANES, 2 * LANES), jnp.bfloat16),
        ),
        4 * 10**9,
        in_specs=[whole, whole, pl.BlockSpec(memory_space=pltpu.SMEM), whole],
        name="observe",
    )(obs_cells, obs_values, live_windows, weighting)
    path, end = call(
        lambda *refs: forward_kernel(rows, blocks, steps, *refs),
        (shape((steps, fields, frame, cols), f32), shape((fields, rows, cols), f32)),
        2 * 10**9,
        name="forward",
    )(start_states, above, below, counts)
    previous_end = lax.ppermute(end, "win", [(i, i + 1) for i in range(windows - 1)])
    own, to_next, to_prev = call(
        lambda *refs: adjoint_kernel(rows, blocks, steps, *refs),
        (
            shape((fields, rows, cols), f32),
            shape((fields, 4, cols), f32),
            shape((fields, 4, cols), f32),
        ),
        4 * 10**9,
        scratch=[pltpu.VMEM((steps, fields, frame, cols), f32)],
        name="adjoint",
    )(path, end, next_start, counts, sums, weights)
    from_prev = lax.ppermute(to_next, "strip", up)
    from_next = lax.ppermute(to_prev, "strip", down)
    gradient, analysis = call(
        lambda *refs: final_kernel(rows, blocks, *refs),
        (shape(start_states.shape, f32), shape(start_states.shape, f32)),
        10**9,
        name="final",
    )(start_states, previous_end, own, from_prev, from_next, weights)
    return gradient, analysis


def solution(mesh):
    placed = (
        P("win", None, "strip", None),
        P("win", None, "strip"),
        P("win", None, "strip"),
        P(),
        P("win"),
    )
    return jax.shard_map(
        per_device,
        mesh=mesh,
        in_specs=placed,
        out_specs=(P("win", None, "strip", None), P("win", None, "strip", None)),
        check_vma=False,
    )
```

time: 107 us -> 43.4 us (0.41)
  local copies, waits for them, and re-layouts: 41.1 us -> 3.26 us
  other arithmetic: 20.4 us -> 0 us
  waiting for transfers between devices: 19.7 us -> 12.7 us
  Pallas kernels: 0 us -> 4.66 us
  between operations: 2.92 us -> 1.38 us
    slice x47 -> x1, local copies, waits for them, and re-layouts: 13.6 us -> 0.96 us  [per_device(): below = lax.ppermute(state[:, :4], 'strip', down)]
    unnamed x117 -> x8, local copies, waits for them, and re-layouts: 13.6 us -> 2.3 us
    scatter-add x6 -> x0, other arithmetic: 8.25 us -> none  [the longest x4 8.19 us: forcing(): target = target.at[cells + write_rows * cols].add(innovation)]
    ppermute x6, waiting for transfers between devices: 19.7 us -> 12.7 us  [the longest x1 8.68 us: per_device(): lax.ppermute(end, 'win', [(i, i + 1) for i in range(windows - 1)])]
    gather x4 -> x0, local copies, waits for them, and re-layouts: 6.88 us -> none  [forcing(): innovation = (source[cells + read_rows * cols] - values) * alive]
    split x72 -> x0, local copies, waits for them, and re-layouts: 6.81 us -> none  [the longest x48 3.73 us: col_diff(): return (jnp.roll(field[1:-1], -1, 1) - jnp.roll(field[1:-1], 1, 1)) * 0.5]
    pallas_call x0 -> x4, Pallas kernels: none -> 4.66 us  [the longest x1 2.06 us: per_device(): call(lambda *refs: adjoint_kernel(rows, blocks, steps, *refs), (shape((fi...]
    add_any x40 -> x0, other arithmetic: 3.63 us -> none  [the longest x32 2.63 us: col_diff(): return (jnp.roll(field[1:-1], -1, 1) - jnp.roll(field[1:-1], 1, 1)) * 0.5]
  transfers between devices with their start and end apart: 6 -> 6, of which waited for: 4 -> 3; matrix products, arithmetic and copies ran while one was open for 21% -> 2% of each run, Pallas kernels for 0% -> 9%
where the time goes in v1:
time: 43.4 us; the launch traced here: 43 us
  starting transfers between devices  21.1 us (49%)
  waiting for transfers between devices  12.7 us (29%)
  Pallas kernels  4.66 us (11%)
  local copies, waits for them, and re-layouts  3.26 us (8%)
  between operations  1.38 us (3%)
    ppermute x1, starting transfers between devices, per_device(): lax.ppermute(state, 'win', [(i + 1, i) for i in range(windows - 1)])  8.74 us
    ppermute x1, waiting for transfers between devices, per_device(): lax.ppermute(end, 'win', [(i, i + 1) for i in range(windows - 1)])  8.68 us
    ppermute x1, waiting for transfers between devices, per_device(): from_next = lax.ppermute(to_prev, 'strip', down)  3.47 us
    ppermute x1, starting transfers between devices, per_device(): from_prev = lax.ppermute(to_next, 'strip', up)  2.91 us
    ppermute x1, starting transfers between devices, per_device(): below = lax.ppermute(state[:, :4], 'strip', down)  2.86 us
    ppermute x1, starting transfers between devices, per_device(): above = lax.ppermute(state[:, rows - 4:], 'strip', up)  2.7 us
    unnamed x8, local copies, waits for them, and re-layouts  2.3 us
    pallas_call x1, Pallas kernels, per_device(): call(lambda *refs: adjoint_kernel(rows, blocks, steps, *refs), (shape((fi...  2.06 us
  transfers between devices with their start and end apart: 6, of which 3 were waited for; matrix products, arithmetic and copies ran while one was open for 2% of the time, Pallas kernels for 9%

profile of v1, /device:TPU:257, one launch (start us, length us, event | category | flops | bytes accessed | tf_op | source)
XLA Modules:
  0.0 43.0 jit_solution(8412898251463370107)
XLA Ops:
  0.6 8.7 %collective-permute-start.3 = (f32[3,16,1024]{2,1,0:T(8,128)}, f32[3,16,1024]{2,1,0:T(8,128)S(1)}, u32[]{:S(2)}, u32[]{:S(2)}) collective-permute-start(f32[3,16,1024]{2,1,0:T(8,128)} %bitcast.1), channel_id=1, source_target_pairs={{8,0},{16,8},{24,16},{32,24},{40,32},{48,40},{56,48},{64,56},{72,6... | collective-permute-start | bytes 589832 | tf_op jit(solution)/shard_map/ppermute | solution.py:295
  9.4 1.0 %fusion = (f32[3,4,1024]{2,1,0:T(4,128)S(1)}, f32[3,4,1024]{2,1,0:T(4,128)S(1)}) fusion(f32[3,16,1024]{2,1,0:T(8,128)} %bitcast.2), kind=kLoop, calls=%fused_computation | loop fusion | bytes 196608 | tf_op jit(solution)/shard_map/slice | solution.py:297
  10.3 2.9 %collective-permute-start.1 = (f32[3,4,1024]{2,1,0:T(4,128)S(1)}, f32[3,4,1024]{2,1,0:T(4,128)S(1)}, u32[]{:S(2)}, u32[]{:S(2)}) collective-permute-start(f32[3,4,1024]{2,1,0:T(4,128)S(1)} %get-tuple-element.18), channel_id=1, source_target_pairs={{1,0},{2,1},{3,2},{4,3},{5,4},{6,5},{7,6},{9,8},{10,9},{11,10},{12... | collective-permute-start | bytes 147464 | tf_op jit(solution)/shard_map/ppermute | solution.py:297
  13.2 2.7 %collective-permute-start = (f32[3,4,1024]{2,1,0:T(4,128)S(1)}, f32[3,4,1024]{2,1,0:T(4,128)S(1)}, u32[]{:S(2)}, u32[]{:S(2)}) collective-permute-start(f32[3,4,1024]{2,1,0:T(4,128)S(1)} %get-tuple-element.19), channel_id=1, source_target_pairs={{0,1},{1,2},{2,3},{3,4},{4,5},{5,6},{6,7},{8,9},{9,10},{10,11},{11... | collective-permute-start | bytes 147464 | tf_op jit(solution)/shard_map/ppermute | solution.py:296
  16.6 0.0 copy-start.1
  16.6 0.9 %copy-done.1 = f32[3,128,128]{2,1,0:T(8,128)S(1)} copy-done((f32[3,128,128]{2,1,0:T(8,128)S(1)}, f32[3,128,128]{2,1,0:T(8,128)}, u32[]{:S(2)}) %copy-start.1) | copy-done | bytes 196632
  17.5 0.0 copy-start.2
  17.5 0.7 %copy-done.2 = s32[1,4,256]{2,1,0:T(4,128)S(1)} copy-done((s32[1,4,256]{2,1,0:T(4,128)S(1)}, s32[1,4,256]{2,1,0:T(4,128)}, u32[]{:S(2)}) %copy-start.2) | copy-done | bytes 4120
  18.2 0.0 copy-start.3
  18.2 0.7 %copy-done.3 = f32[1,4,256]{2,1,0:T(4,128)S(1)} copy-done((f32[1,4,256]{2,1,0:T(4,128)S(1)}, f32[1,4,256]{2,1,0:T(4,128)}, u32[]{:S(2)}) %copy-start.3) | copy-done | bytes 4120
  18.9 0.0 copy-start
  18.9 0.5 %observe.1 = (f32[4,16,1024]{2,1,0:T(8,128)S(1)}, f32[4,16,1024]{2,1,0:T(8,128)S(1)}, bf16[3,128,256]{2,1,0:T(8,128)(2,1)S(1)}) custom-call(s32[1,4,256]{2,1,0:T(4,128)S(1)} %copy-done.2, f32[1,4,256]{2,1,0:T(4,128)S(1)} %copy-done.3, s32[1]{0:T(128)S(6)} %copy.7.refs_2_, f32[3,128,128]{2,1,0:T(8,128)S(1)} %copy-done.1), custom_call_target="tpu_custom_call" | custom-call | flops 4000000000 | bytes 1000000 | tf_op jit(solution)/shard_map/observe/pallas_call | solution.py:300
  19.3 0.5 %collective-permute-done.1.refs_2_ = f32[3,4,1024]{2,1,0:T(4,128)S(1)} collective-permute-done((f32[3,4,1024]{2,1,0:T(4,128)S(1)}, f32[3,4,1024]{2,1,0:T(4,128)S(1)}, u32[]{:S(2)}, u32[]{:S(2)}) %collective-permute-start.1) | collective-permute-done | bytes 49184 | tf_op jit(solution)/shard_map/ppermute | solution.py:297
  19.9 0.0 collective-permute-done.refs_1_
  19.9 0.0 copy-done
  19.9 1.1 %forward.1 = (f32[4,3,24,1024]{3,2,1,0:T(8,128)S(1)}, f32[3,16,1024]{2,1,0:T(8,128)S(1)}) custom-call(f32[1,3,16,1024]{3,2,1,0:T(8,128)S(1)} %copy-done, f32[3,4,1024]{2,1,0:T(4,128)S(1)} %collective-permute-done.refs_1_, f32[3,4,1024]{2,1,0:T(4,128)S(1)} %collective-permute-done.1.refs_2_, f32[4,16,1024]{2,1,0:T(8,128)S(1)} %get-tuple-element.10.refs_3_), custom_call_target="tpu_custom_call" | custom-call | flops 2000000000 | bytes 1000000 | tf_op jit(solution)/shard_map/forward/pallas_call | solution.py:311
  21.0 1.9 %collective-permute-start.2 = (f32[3,16,1024]{2,1,0:T(8,128)S(1)}, f32[3,16,1024]{2,1,0:T(8,128)S(1)}, u32[]{:S(2)}, u32[]{:S(2)}) collective-permute-start(f32[3,16,1024]{2,1,0:T(8,128)S(1)} %get-tuple-element.11.refs_1_), channel_id=1, source_target_pairs={{0,8},{8,16},{16,24},{24,32},{32,40},{40,48},{48,56},{56,64},{64,7... | collective-permute-start | bytes 589832 | tf_op jit(solution)/shard_map/ppermute | solution.py:317
  22.9 0.0 collective-permute-done.3.refs_2_
  23.0 2.1 %adjoint.1 = (f32[3,16,1024]{2,1,0:T(8,128)S(1)}, f32[3,4,1024]{2,1,0:T(4,128)S(1)}, f32[3,4,1024]{2,1,0:T(4,128)S(1)}) custom-call(f32[4,3,24,1024]{3,2,1,0:T(8,128)S(1)} %get-tuple-element.12.refs_0_, f32[3,16,1024]{2,1,0:T(8,128)S(1)} %get-tuple-element.11.refs_1_, f32[3,16,1024]{2,1,0:T(8,128)S(1)} %collective-permute-done.3.refs_2_, ...), custom_call_target="tpu_custom_call" | custom-call | flops 4000000000 | bytes 1000000 | tf_op jit(solution)/shard_map/adjoint/pallas_call | solution.py:318
  25.0 2.9 %collective-permute-start.4 = (f32[3,4,1024]{2,1,0:T(4,128)S(1)}, f32[3,4,1024]{2,1,0:T(4,128)S(1)}, u32[]{:S(2)}, u32[]{:S(2)}) collective-permute-start(f32[3,4,1024]{2,1,0:T(4,128)S(1)} %get-tuple-element.16), channel_id=1, source_target_pairs={{0,1},{1,2},{2,3},{3,4},{4,5},{5,6},{6,7},{8,9},{9,10},{10,11},{11... | collective-permute-start | bytes 147464 | tf_op jit(solution)/shard_map/ppermute | solution.py:329
  27.9 1.9 %collective-permute-start.5 = (f32[3,4,1024]{2,1,0:T(4,128)S(1)}, f32[3,4,1024]{2,1,0:T(4,128)S(1)}, u32[]{:S(2)}, u32[]{:S(2)}) collective-permute-start(f32[3,4,1024]{2,1,0:T(4,128)S(1)} %get-tuple-element.17), channel_id=1, source_target_pairs={{1,0},{2,1},{3,2},{4,3},{5,4},{6,5},{7,6},{9,8},{10,9},{11,10},{12... | collective-permute-start | bytes 147464 | tf_op jit(solution)/shard_map/ppermute | solution.py:330
  29.9 0.0 collective-permute-done.4.refs_3_
  29.9 3.5 %collective-permute-done.5.refs_4_ = f32[3,4,1024]{2,1,0:T(4,128)S(1)} collective-permute-done((f32[3,4,1024]{2,1,0:T(4,128)S(1)}, f32[3,4,1024]{2,1,0:T(4,128)S(1)}, u32[]{:S(2)}, u32[]{:S(2)}) %collective-permute-start.5) | collective-permute-done | bytes 49184 | tf_op jit(solution)/shard_map/ppermute | solution.py:330
  33.3 8.7 %collective-permute-done.2.refs_1_ = f32[3,16,1024]{2,1,0:T(8,128)S(1)} collective-permute-done((f32[3,16,1024]{2,1,0:T(8,128)S(1)}, f32[3,16,1024]{2,1,0:T(8,128)S(1)}, u32[]{:S(2)}, u32[]{:S(2)}) %collective-permute-start.2) | collective-permute-done | bytes 196640 | tf_op jit(solution)/shard_map/ppermute | solution.py:317
  42.0 1.0 %final.1 = (f32[1,3,16,1024]{3,2,1,0:T(8,128)}, f32[1,3,16,1024]{3,2,1,0:T(8,128)}) custom-call(f32[1,3,16,1024]{3,2,1,0:T(8,128)S(1)} %copy-done, f32[3,16,1024]{2,1,0:T(8,128)S(1)} %collective-permute-done.2.refs_1_, f32[3,16,1024]{2,1,0:T(8,128)S(1)} %get-tuple-element.15.refs_2_, f32[3,4,1024]{2,1,0:T(4,128)S(1)} %collective-permute-done.4.refs_3_, ...), custom_call_target="tpu_custom_call" | custom-call | flops 1000000000 | bytes 1000000 | tf_op jit(solution)/shard_map/final/pallas_call | solution.py:331
Async XLA Ops:
  0.6 22.3 %collective-permute-start.3 = (f32[3,16,1024]{2,1,0:T(8,128)}, f32[3,16,1024]{2,1,0:T(8,128)S(1)}, u32[]{:S(2)}, u32[]{:S(2)}) collective-permute-start(f32[3,16,1024]{2,1,0:T(8,128)} %bitcast.1), channel_id=1, source_target_pairs={{8,0},{16,8},{24,16},{32,24},{40,32},{48,40},{56,48},{64,56},{72,6... | collective-permute-start | bytes 589832 | tf_op jit(solution)/shard_map/ppermute | solution.py:295
  10.3 9.5 %collective-permute-start.1 = (f32[3,4,1024]{2,1,0:T(4,128)S(1)}, f32[3,4,1024]{2,1,0:T(4,128)S(1)}, u32[]{:S(2)}, u32[]{:S(2)}) collective-permute-start(f32[3,4,1024]{2,1,0:T(4,128)S(1)} %get-tuple-element.18), channel_id=1, source_target_pairs={{1,0},{2,1},{3,2},{4,3},{5,4},{6,5},{7,6},{9,8},{10,9},{11,10},{12... | collective-permute-start | bytes 147464 | tf_op jit(solution)/shard_map/ppermute | solution.py:297
  13.2 6.7 %collective-permute-start = (f32[3,4,1024]{2,1,0:T(4,128)S(1)}, f32[3,4,1024]{2,1,0:T(4,128)S(1)}, u32[]{:S(2)}, u32[]{:S(2)}) collective-permute-start(f32[3,4,1024]{2,1,0:T(4,128)S(1)} %get-tuple-element.19), channel_id=1, source_target_pairs={{0,1},{1,2},{2,3},{3,4},{4,5},{5,6},{6,7},{8,9},{9,10},{10,11},{11... | collective-permute-start | bytes 147464 | tf_op jit(solution)/shard_map/ppermute | solution.py:296
  16.6 0.9 %copy-start.1 = (f32[3,128,128]{2,1,0:T(8,128)S(1)}, f32[3,128,128]{2,1,0:T(8,128)}, u32[]{:S(2)}) copy-start(f32[3,128,128]{2,1,0:T(8,128)} %refs_3_.1) | copy-start | bytes 589828
  17.5 0.7 %copy-start.2 = (s32[1,4,256]{2,1,0:T(4,128)S(1)}, s32[1,4,256]{2,1,0:T(4,128)}, u32[]{:S(2)}) copy-start(s32[1,4,256]{2,1,0:T(4,128)} %refs_0_.3) | copy-start | bytes 12292
  18.2 0.7 %copy-start.3 = (f32[1,4,256]{2,1,0:T(4,128)S(1)}, f32[1,4,256]{2,1,0:T(4,128)}, u32[]{:S(2)}) copy-start(f32[1,4,256]{2,1,0:T(4,128)} %refs_1_.1) | copy-start | bytes 12292
  18.9 1.0 %copy-start = (f32[1,3,16,1024]{3,2,1,0:T(8,128)S(1)}, f32[1,3,16,1024]{3,2,1,0:T(8,128)}, u32[]{:S(2)}) copy-start(f32[1,3,16,1024]{3,2,1,0:T(8,128)} %refs_0_.5) | copy-start | bytes 589828
  21.0 21.0 %collective-permute-start.2 = (f32[3,16,1024]{2,1,0:T(8,128)S(1)}, f32[3,16,1024]{2,1,0:T(8,128)S(1)}, u32[]{:S(2)}, u32[]{:S(2)}) collective-permute-start(f32[3,16,1024]{2,1,0:T(8,128)S(1)} %get-tuple-element.11.refs_1_), channel_id=1, source_target_pairs={{0,8},{8,16},{16,24},{24,32},{32,40},{40,48},{48,56},{56,64},{64,7... | collective-permute-start | bytes 589832 | tf_op jit(solution)/shard_map/ppermute | solution.py:317
  25.0 4.8 %collective-permute-start.4 = (f32[3,4,1024]{2,1,0:T(4,128)S(1)}, f32[3,4,1024]{2,1,0:T(4,128)S(1)}, u32[]{:S(2)}, u32[]{:S(2)}) collective-permute-start(f32[3,4,1024]{2,1,0:T(4,128)S(1)} %get-tuple-element.16), channel_id=1, source_target_pairs={{0,1},{1,2},{2,3},{3,4},{4,5},{5,6},{6,7},{8,9},{9,10},{10,11},{11... | collective-permute-start | bytes 147464 | tf_op jit(solution)/shard_map/ppermute | solution.py:329
  27.9 5.4 %collective-permute-start.5 = (f32[3,4,1024]{2,1,0:T(4,128)S(1)}, f32[3,4,1024]{2,1,0:T(4,128)S(1)}, u32[]{:S(2)}, u32[]{:S(2)}) collective-permute-start(f32[3,4,1024]{2,1,0:T(4,128)S(1)} %get-tuple-element.17), channel_id=1, source_target_pairs={{1,0},{2,1},{3,2},{4,3},{5,4},{6,5},{7,6},{9,8},{10,9},{11,10},{12... | collective-permute-start | bytes 147464 | tf_op jit(solution)/shard_map/ppermute | solution.py:330
